TPU v7x, 32 devices: a whole 2x2x4 slice. The times are simulated.
32 devices in a mesh: seq: 8 (over y, x, core), head: 4 (over z).
Axes of the slice: x: 2, y: 2, z: 4, core: 2. Of those that a mesh axis runs over, the one named last changes fastest.
Arguments:
- latent_cache: bfloat16 [2, 16384, 576], P(None, 'seq'), may hold values from -8 to 8
- draft_latent: bfloat16 [2, 64, 576], P(None, 'seq'), may hold values from -9 to 9
- query_nope: bfloat16 [2, 64, 128, 128], P(None, None, 'head'), may hold values from -6 to 6
- query_rope: bfloat16 [2, 64, 128, 64], P(None, None, 'head'), may hold values from -8 to 8
- parents: int32 [2, 64], replicated, may hold values from -1 to 62, as said below
- lengths: int32 [2], replicated, may hold values from 8192 to 16384
- key_weight: bfloat16 [128, 128, 512], P('head'), may hold values from -0.25 to 0.25
- value_weight: bfloat16 [128, 512, 128], P('head'), may hold values from -0.25 to 0.25
- out_weight: bfloat16 [16384, 7168], P('head', 'seq'), may hold values from -0.046875 to 0.046875
- residual: bfloat16 [2, 64, 7168], P(None, None, 'seq'), may hold values from -40 to 40
- norm_gain: bfloat16 [7168], P('seq'), may hold values from 0.5 to 1.5
- vocab_weight: bfloat16 [7168, 8192], P('seq', 'head'), may hold values from -0.21875 to 0.21875
Outputs:
- logits: bfloat16 [2, 64, 8192], P(None, None, ('head', 'seq'))
Inputs may be any that keep to these rules, and one draw needn't show every extreme that they name: `parents`: token 0 is the root of each tree with parent -1; every other token's parent is an earlier token; the last token's parent is the token just before it.
All inputs are finite; a program needn't handle non-finite values.
Results may differ from a plain program's by a relative error of at most 0.02.
Values may be sent and summed in bfloat16 or wider, within the bound.
No kernel may reach another device: no remote copies, remote signals or barrier semaphores. Data moves between devices by JAX's collectives and lax.ppermute only.
A program may use at most 128 MiB of HBM per device.

v0:
```python
import math
import jax
import jax.numpy as jnp
from jax import lax
from jax.sharding import PartitionSpec as P

D = 7168
NEGATIVE = -1e30
EPSILON = 1e-06


def ancestry_of(parents):
    token_count = parents.shape[1]
    indices = jnp.arange(token_count, dtype=jnp.int32)
    linked = (parents[:, :, None] == indices[None, None, :]) | (
        indices[:, None] == indices[None, :]
    )[None]
    reachable = linked.astype(jnp.float32)
    for repeat in range(max(1, (token_count - 1).bit_length())):
        product = jnp.einsum("bij,bjk->bik", reachable, reachable, precision=lax.Precision.HIGHEST)
        reachable = jnp.where(product > 0.5, 1.0, 0.0).astype(jnp.float32)
    return reachable


def per_device(
    latent_cache,
    draft_latent,
    query_nope,
    query_rope,
    parents,
    lengths,
    key_weight,
    value_weight,
    out_weight,
    residual,
    norm_gain,
    vocab_weight,
):
    requests, cache_local, width = latent_cache.shape
    latent = value_weight.shape[1]
    heads_local = key_weight.shape[0]
    drafted = query_nope.shape[1]
    draft_local = draft_latent.shape[1]
    scaling = 1.0 / math.sqrt(query_nope.shape[3] + query_rope.shape[3])
    seat = lax.axis_index("seq")
    absorbed = jnp.einsum(
        "bthn,hnl->bthl", query_nope, key_weight, preferred_element_type=jnp.float32
    ).astype(jnp.bfloat16)
    queries = jnp.concatenate([absorbed, query_rope], axis=-1)
    ancestry = ancestry_of(parents)
    own_tree = lax.dynamic_slice_in_dim(ancestry, seat * draft_local, draft_local, 2)
    positions = seat * cache_local + jnp.arange(cache_local, dtype=jnp.int32)
    live = positions[None, :] < lengths[:, None]
    cache_values = latent_cache[:, :, :latent]
    draft_values = draft_latent[:, :, :latent]
    row_count = drafted * heads_local
    block = queries.reshape(requests, row_count, width)
    tree_block = own_tree
    tree_block = jnp.broadcast_to(
        tree_block[:, :, None, :], (requests, drafted, heads_local, draft_local)
    )
    tree_block = tree_block.reshape(requests, row_count, draft_local)
    cache_scores = (
        jnp.einsum("brc,bkc->brk", block, latent_cache, preferred_element_type=jnp.float32)
        * scaling
    )
    cache_scores = jnp.where(live[:, None, :], cache_scores, NEGATIVE)
    draft_scores = (
        jnp.einsum("brc,bkc->brk", block, draft_latent, preferred_element_type=jnp.float32)
        * scaling
    )
    draft_scores = jnp.where(tree_block > 0.5, draft_scores, NEGATIVE)
    cache_scores, draft_scores, tree_block = (cache_scores, draft_scores, tree_block)
    local_max = jnp.maximum(jnp.max(cache_scores, -1), jnp.max(draft_scores, -1))
    row_max = lax.pmax(local_max, "seq")
    cache_weights = jnp.where(live[:, None, :], jnp.exp(cache_scores - row_max[..., None]), 0.0)
    draft_weights = jnp.where(tree_block > 0.5, jnp.exp(draft_scores - row_max[..., None]), 0.0)
    total = jnp.sum(cache_weights, -1) + jnp.sum(draft_weights, -1)
    mixed = jnp.einsum(
        "brk,bkl->brl",
        cache_weights.astype(jnp.bfloat16),
        cache_values,
        preferred_element_type=jnp.float32,
    )
    mixed = mixed + jnp.einsum(
        "brk,bkl->brl",
        draft_weights.astype(jnp.bfloat16),
        draft_values,
        preferred_element_type=jnp.float32,
    )
    total, mixed = (total, mixed)
    own_total, own_mixed = (
        lax.psum_scatter(total.astype(jnp.bfloat16), "seq", scatter_dimension=1, tiled=True).astype(
            jnp.float32
        ),
        lax.psum_scatter(mixed.astype(jnp.bfloat16), "seq", scatter_dimension=1, tiled=True).astype(
            jnp.float32
        ),
    )
    latent_out = (own_mixed / own_total[..., None]).astype(jnp.bfloat16)
    latent_out = latent_out.reshape(requests, draft_local, heads_local, latent)
    per_head = jnp.einsum(
        "bthl,hlv->bthv", latent_out, value_weight, preferred_element_type=jnp.float32
    ).astype(jnp.bfloat16)
    head_values = per_head.reshape(requests, draft_local, heads_local * value_weight.shape[2])
    attention = jnp.dot(
        lax.all_gather(head_values, "seq", axis=1, tiled=True),
        out_weight,
        preferred_element_type=jnp.float32,
    )
    attention = lax.psum(attention.astype(jnp.bfloat16), "head").astype(jnp.float32)
    hidden = residual.astype(jnp.float32) + attention
    squares = lax.psum(jnp.sum(hidden * hidden, -1), "seq")
    normed = (
        hidden * lax.rsqrt(squares / D + EPSILON)[..., None] * norm_gain.astype(jnp.float32)
    ).astype(jnp.bfloat16)
    partial_logits = jnp.dot(normed, vocab_weight, preferred_element_type=jnp.float32)
    return lax.psum_scatter(
        partial_logits.astype(jnp.bfloat16), "seq", scatter_dimension=2, tiled=True
    )


def solution(mesh):
    in_specs = (
        P(None, "seq", None),
        P(None, "seq", None),
        P(None, None, "head", None),
        P(None, None, "head", None),
        P(),
        P(),
        P("head", None, None),
        P("head", None, None),
        P("head", "seq"),
        P(None, None, "seq"),
        P("seq"),
        P("seq", "head"),
    )
    out_specs = P(None, None, ("head", "seq"))
    return jax.shard_map(
        per_device, mesh=mesh, in_specs=in_specs, out_specs=out_specs, check_vma=False
    )
```

profile of v0, /device:TPU:0, one launch (start us, length us, event | category | flops | bytes accessed | tf_op | source)
XLA Modules:
  0.0 305.8 jit_solution(1082863160173444389)
XLA Ops:
  6.6 1.0 fusion.43
  7.9 0.2 fusion.45
  8.1 0.2 fusion.46
  8.4 0.2 fusion.47
  9.1 0.3 gt.33
  9.4 1.6 copy.41
  11.0 3.4 %fusion.101 = f32[32,512,128]{1,2,0:S(1)} fusion(bf16[32,128,128]{1,2,0:T(8,128)(2,1)S(1)} %bitcast.49, bf16[32,128,512]{2,1,0:T(8,128)(2,1)} %param.18), kind=kOutput, calls=%fused_computation.115 | convolution fusion | flops 536870912 | bytes 13631488
  14.4 0.7 convert_bitcast_fusion
  15.1 0.6 copy-done.1
  15.7 0.4 copy.42
  16.1 0.8 pad_maximum_fusion
  16.9 5.4 %copy.43 = bf16[2,64,32,576]{3,2,1,0:T(8,128)(2,1)} copy(bf16[2,64,32,576]{3,1,0,2:T(8,128)(2,1)S(1)} %pad_maximum_fusion) | data formatting | bytes 9437184 | tf_op jit(solution)/shard_map/concatenate | solution.py:49
  22.5 4.0 %fusion.100 = (f32[2,2048]{1,0:T(2,128)S(1)}, f32[2,2048,8]{1,2,0:T(8,128)S(1)}) fusion(pred[2,2048,8]{1,2,0:T(8,128)(4,1)S(1)} %gt.33, bf16[2,2048,576]{2,1,0:T(8,128)(2,1)} %bitcast.47, bf16[2,8,576]{2,1,0:T(8,128)(2,1)S(1)} %copy-done.2), kind=kOutput, calls=%fused_computation.114 | convolution fusion | flops 37842944 | bytes 4917248 | tf_op jit(solution)/shard_map/brc,bkc->brk/dot_general | solution.py:69
  26.4 23.1 %fusion = (f32[2,2048]{1,0:T(2,128)S(1)}, f32[2,2048,2048]{1,2,0:T(8,128)}) fusion(pred[2,2048]{1,0:T(4,128)(4,1)S(1)} %broadcast_compare_fusion, bf16[2,2048,576]{2,1,0:T(8,128)(2,1)} %bitcast.48, bf16[2,2048,576]{1,2,0:T(8,128)(2,1)} %param.12), kind=kOutput, calls=%fused_computation.2 | convolution fusion | flops 9688838144 | bytes 43012096 | tf_op jit(solution)/shard_map/brc,bkc->brk/dot_general | solution.py:64
  49.5 25.5 %pmax.7 = f32[2,2048]{1,0:T(2,128)S(1)} all-reduce(f32[2,2048]{1,0:T(2,128)S(1)} %max.5), channel_id=1, replica_groups=mesh['seq'=8,'head'=4] {'seq'}, use_global_device_ids=true, to_apply=%region_2.3 | all-reduce | flops 4096 | bytes 32768 | tf_op jit(solution)/shard_map/pmax | solution.py:75
  75.2 15.7 %fusion.1 = f32[2,2048]{1,0:T(2,128)S(1)} fusion(f32[2,2048,2048]{1,2,0:T(8,128)} %get-tuple-element.6, f32[2,2048]{1,0:T(2,128)S(1)} %pmax.7, pred[2,2048]{1,0:T(4,128)(4,1)S(1)} %broadcast_compare_fusion), kind=kLoop, calls=%fused_computation.3 | loop fusion | flops 41938944 | bytes 33591296 | tf_op jit(solution)/shard_map/reduce_sum | solution.py:78
  90.9 1.1 copy.82
  92.0 1.3 fusion.53
  93.3 23.2 %add_convert_fusion = bf16[2,2048,512]{2,1,0:T(8,128)(2,1)} fusion(f32[2,2048,512]{2,1,0:T(8,128)S(1)} %fusion.53, f32[2,2048,2048]{1,2,0:T(8,128)} %get-tuple-element.6, f32[2,2048]{1,0:T(2,128)S(1)} %pmax.7, pred[2,2048]{1,0:T(4,128)(4,1)S(1)} %broadcast_compare_fusion, bf16[2,2048,576]{1,2,0:T(8,128)(2,1)} %param.12), kind=kOutput, calls=%fused_computation.7 | convolution fusion | flops 8636071936 | bytes 50352128 | tf_op jit(solution)/shard_map/brk,bkl->brl/dot_general | solution.py:79
  116.6 9.0 %reduce-scatter.10.cloned.1.call-done = bf16[256,2]{1,0:T(8,128)(2,1)} async-done(((bf16[2048,2]{1,0:T(8,128)(2,1)}), bf16[256,2]{1,0:T(8,128)(2,1)}) %reduce-scatter.10.cloned.1.call-update) | async-done | bytes 1040
  125.6 0.9 copy.83
  126.5 53.5 %reduce-scatter.6.cloned.1.call-done = bf16[2,256,512]{2,1,0:T(8,128)(2,1)} async-done(((bf16[2,2048,512]{2,1,0:T(8,128)(2,1)}), bf16[2,256,512]{2,1,0:T(8,128)(2,1)}) %reduce-scatter.6.cloned.1.call-update) | async-done | bytes 524304 | tf_op jit(solution)/shard_map/reduce_scatter | solution.py:96
  180.1 1.2 divide_convert_fusion
  181.4 3.1 %fusion.25 = bf16[32,2,1,8,128]{4,3,2,1,0:T(8,128)(2,1)S(1)} fusion(bf16[32,512,128]{2,1,0:T(8,128)(2,1)} %param.19, bf16[2,8,32,512]{3,2,1,0:T(8,128)(2,1)S(1)} %bitcast.50), kind=kOutput, calls=%fused_computation.22 | convolution fusion | flops 67174400 | bytes 4849664 | tf_op jit(solution)/shard_map/bthl,hlv->bthv/dot_general | solution.py:102
  184.4 0.7 copy.89
  185.2 23.5 %all-gather.2.cloned.1.call-done = bf16[2,64,4096]{2,1,0:T(8,128)(2,1)} async-done(((bf16[2,8,4096]{2,1,0:T(8,128)(2,1)}), bf16[2,64,4096]{2,1,0:T(8,128)(2,1)}) %all-gather.2.cloned.1.call-update) | async-done | bytes 1048592 | tf_op jit(solution)/shard_map/all_gather | solution.py:107
  208.7 5.4 %fusion.19 = bf16[2,64,896]{2,1,0:T(8,128)(2,1)} fusion(bf16[2,64,4096]{2,1,0:T(8,128)(2,1)} %all-gather.2.cloned.1.call-done, bf16[4096,896]{1,0:T(8,128)(2,1)} %param.20), kind=kOutput, calls=%fused_computation.20 | convolution fusion | flops 939638784 | bytes 8617984 | tf_op jit(solution)/shard_map/dot_general | solution.py:106
  214.1 35.3 %all-reduce.2.cloned.1.call-done = bf16[2,64,896]{2,1,0:T(8,128)(2,1)} async-done(((bf16[2,64,896]{2,1,0:T(8,128)(2,1)}), bf16[2,64,896]{2,1,0:T(8,128)(2,1)}) %all-reduce.2.cloned.1.call-update) | async-done | bytes 229392 | tf_op jit(solution)/shard_map/psum | solution.py:111
  249.4 1.1 multiply_reduce_fusion
  250.5 11.8 %psum.15 = f32[2,64]{1,0:T(2,128)S(1)} all-reduce(f32[2,64]{1,0:T(2,128)S(1)} %multiply_reduce_fusion), channel_id=1, replica_groups=mesh['seq'=8,'head'=4] {'seq'}, use_global_device_ids=true, to_apply=%region_9.10 | all-reduce | flops 128 | bytes 1024 | tf_op jit(solution)/shard_map/psum | solution.py:113
  262.3 3.8 %fusion.15 = bf16[2,64,2048]{2,1,0:T(8,128)(2,1)} fusion(bf16[896,2048]{1,0:T(8,128)(2,1)} %param.23, bf16[2,64,896]{2,1,0:T(8,128)(2,1)} %all-reduce.2.cloned.1.call-done, bf16[2,64,896]{2,1,0:T(8,128)(2,1)S(1)} %copy-done, f32[896]{0:T(1024)S(1)} %convert_element_type.66, f32[2,64]{1,0:T(2,128)S(1)} %add_rsqrt_fusion), kind=kOutput, calls=%fused_computation.17 | convolution fusion | flops 470712320 | bytes 4657152 | tf_op jit(solution)/shard_map/dot_general | solution.py:117
  266.1 33.1 %reduce-scatter.8.cloned.1.call-done = bf16[2,64,256]{2,1,0:T(8,128)(2,1)} async-done(((bf16[2,64,2048]{2,1,0:T(8,128)(2,1)}), bf16[2,64,256]{2,1,0:T(8,128)(2,1)}) %reduce-scatter.8.cloned.1.call-update) | async-done | bytes 65552 | tf_op jit(solution)/shard_map/reduce_scatter | solution.py:118
  (37 shorter events, 1.3 us)
Async XLA Ops:
  6.5 119.1 %reduce-scatter.10.cloned.1.call-start = ((), (), s32[]{:S(2)}) async-start(), calls=%async_computation.7 | async-start | bytes 589824
  14.4 1.2 copy-start.1
  16.1 6.3 %copy-start.4 = (s32[2]{0:T(128)S(1)}, s32[2]{0:T(128)}, u32[]{:S(2)}) copy-start(s32[2]{0:T(128)} %param.17) | copy-start | bytes 28
  16.1 6.4 %copy-start.2 = (bf16[2,8,576]{2,1,0:T(8,128)(2,1)S(1)}, bf16[2,8,576]{2,1,0:T(8,128)(2,1)}, u32[]{:S(2)}) copy-start(bf16[2,8,576]{2,1,0:T(8,128)(2,1)} %param.13) | copy-start | bytes 55300
  92.0 88.1 %reduce-scatter.6.cloned.1.call-start = ((), (), s32[]{:S(2)}) async-start(), calls=%async_computation.3 | async-start | bytes 4718592 | tf_op jit(solution)/shard_map/reduce_scatter | solution.py:96
  116.5 92.1 %all-gather.2.cloned.1.call-start = ((), (), s32[]{:S(2)}) async-start(), calls=%async_computation.4 | async-start | bytes 1179648 | tf_op jit(solution)/shard_map/all_gather | solution.py:107
  181.3 32.8 %copy-start.3 = (bf16[896]{0:T(1024)(128)(2,1)S(1)}, bf16[896]{0:T(1024)(128)(2,1)}, u32[]{:S(2)}) copy-start(bf16[896]{0:T(1024)(128)(2,1)} %param.22) | copy-start | bytes 5380
  181.3 68.1 %copy-start = (bf16[2,64,896]{2,1,0:T(8,128)(2,1)S(1)}, bf16[2,64,896]{2,1,0:T(8,128)(2,1)}, u32[]{:S(2)}) copy-start(bf16[2,64,896]{2,1,0:T(8,128)(2,1)} %param.21) | copy-start | bytes 688132
  185.1 64.3 %all-reduce.2.cloned.1.call-start = ((), (), s32[]{:S(2)}) async-start(), calls=%async_computation.5 | async-start | bytes 458752 | tf_op jit(solution)/shard_map/psum | solution.py:111
  214.1 85.2 %reduce-scatter.8.cloned.1.call-start = ((), (), s32[]{:S(2)}) async-start(), calls=%async_computation.6 | async-start | bytes 589824 | tf_op jit(solution)/shard_map/reduce_scatter | solution.py:118
Sparse Core Ops, SparseCore 0:
  92.1 33.5 reduce-scatter.9
  129.0 51.0 reduce-scatter.5
  185.3 23.3 all-gather.1
  214.2 35.1 all-reduce.1
  266.2 32.9 reduce-scatter.7
where the time goes:
time: 306 us
  waiting for transfers between devices  155 us (51%)
  matrix products  69.3 us (23%)
  blocking collectives  37.3 us (12%)
  other arithmetic  19.8 us (6%)
  between operations  13.4 us (4%)
  local copies, waits for them, and re-layouts  11.2 us (4%)
    reduce_scatter x1, waiting for transfers between devices, per_device(): lax.psum_scatter(mixed.astype(jnp.bfloat16), 'seq', scatter_dimension=1,...  53.5 us
    psum x1, waiting for transfers between devices, per_device(): lax.psum(attention.astype(jnp.bfloat16), 'head').astype(jnp.float32)  35.3 us
    reduce_scatter x1, waiting for transfers between devices, per_device(): lax.psum_scatter(partial_logits.astype(jnp.bfloat16), 'seq', scatter_dime...  33.1 us
    pmax x1, blocking collectives, per_device(): row_max = lax.pmax(local_max, 'seq')  25.5 us
    all_gather x1, waiting for transfers between devices, per_device(): lax.all_gather(head_values, 'seq', axis=1, tiled=True)  23.5 us
    dot_general x1, matrix products, per_device(): jnp.einsum('brk,bkl->brl', cache_weights.astype(jnp.bfloat16), cache_valu...  23.2 us
    dot_general x1, matrix products, per_device(): jnp.einsum('brc,bkc->brk', block, latent_cache, preferred_element_type=jn...  23.1 us
    reduce_sum x2, other arithmetic, per_device(): total = jnp.sum(cache_weights, -1) + jnp.sum(draft_weights, -1)  15.8 us
  transfers between devices with their start and end apart: 5, of which 5 were waited for; matrix products, arithmetic and copies ran while one was open for 8% of the time, Pallas kernels for 0%

commit v1 on v0

--- a/solution.py
+++ b/solution.py
@@ -108,7 +108,9 @@
         out_weight,
         preferred_element_type=jnp.float32,
     )
-    attention = lax.psum(attention.astype(jnp.bfloat16), "head").astype(jnp.float32)
+    attention = jnp.sum(
+        lax.all_gather(attention.astype(jnp.bfloat16), axis_name="head"), axis=0
+    ).astype(jnp.float32)
     hidden = residual.astype(jnp.float32) + attention
     squares = lax.psum(jnp.sum(hidden * hidden, -1), "seq")
     normed = (

time: 306 us -> 291 us (0.951)
  waiting for transfers between devices: 155 us -> 120 us
  blocking collectives: 37.3 us -> 58.4 us
    psum x1 -> x0, waiting for transfers between devices: 35.3 us -> none  [per_device(): lax.psum(attention.astype(jnp.bfloat16), 'head').astype(jnp.float32)]
    all_gather x0 -> x1, blocking collectives: none -> 21 us  [per_device(): lax.all_gather(attention.astype(jnp.bfloat16), axis_name='head')]
    unnamed x6 -> x5, waiting for transfers between devices: 9.11 us -> 9.1 us
  transfers between devices with their start and end apart: 5 -> 4, of which waited for: 5 -> 4; matrix products, arithmetic and copies ran while one was open for 8% -> 9% of each run, Pallas kernels for 0% -> 0%
where the time goes in v1:
time: 291 us; the launch traced here: 290 us
  waiting for transfers between devices  120 us (41%)
  matrix products  68.4 us (24%)
  blocking collectives  58.4 us (20%)
  other arithmetic  19 us (7%)
  between operations  13.4 us (5%)
  local copies, waits for them, and re-layouts  11.2 us (4%)
    reduce_scatter x1, waiting for transfers between devices, per_device(): lax.psum_scatter(mixed.astype(jnp.bfloat16), 'seq', scatter_dimension=1,...  53.5 us
    reduce_scatter x1, waiting for transfers between devices, per_device(): lax.psum_scatter(partial_logits.astype(jnp.bfloat16), 'seq', scatter_dime...  33.7 us
    pmax x1, blocking collectives, per_device(): row_max = lax.pmax(local_max, 'seq')  25.5 us
    all_gather x1, waiting for transfers between devices, per_device(): lax.all_gather(head_values, 'seq', axis=1, tiled=True)  23.5 us
    dot_general x1, matrix products, per_device(): jnp.einsum('brk,bkl->brl', cache_weights.astype(jnp.bfloat16), cache_valu...  23.2 us
    dot_general x1, matrix products, per_device(): jnp.einsum('brc,bkc->brk', block, latent_cache, preferred_element_type=jn...  23.1 us
    all_gather x1, blocking collectives, per_device(): lax.all_gather(attention.astype(jnp.bfloat16), axis_name='head')  21 us
    reduce_sum x2, other arithmetic, per_device(): total = jnp.sum(cache_weights, -1) + jnp.sum(draft_weights, -1)  15.8 us
  transfers between devices with their start and end apart: 4, of which 4 were waited for; matrix products, arithmetic and copies ran while one was open for 9% of the time, Pallas kernels for 0%

profile of v1, /device:TPU:0, one launch (start us, length us, event | category | flops | bytes accessed | tf_op | source)
XLA Modules:
  0.0 290.3 jit_solution(8407828024427616928)
XLA Ops:
  6.6 1.0 fusion.43
  7.6 0.2 fusion.44
  7.9 0.2 fusion.45
  8.1 0.2 fusion.46
  8.4 0.2 fusion.47
  9.1 0.3 gt.33
  9.4 1.6 copy.41
  11.0 3.4 %fusion.101 = f32[32,512,128]{1,2,0:S(1)} fusion(bf16[32,128,128]{1,2,0:T(8,128)(2,1)S(1)} %bitcast.50, bf16[32,128,512]{2,1,0:T(8,128)(2,1)} %param.18), kind=kOutput, calls=%fused_computation.115 | convolution fusion | flops 536870912 | bytes 13631488
  14.4 0.7 convert_bitcast_fusion
  15.1 0.6 copy-done.1
  15.7 0.4 copy.42
  16.1 0.8 pad_maximum_fusion
  16.9 5.4 %copy.43 = bf16[2,64,32,576]{3,2,1,0:T(8,128)(2,1)} copy(bf16[2,64,32,576]{3,1,0,2:T(8,128)(2,1)S(1)} %pad_maximum_fusion) | data formatting | bytes 9437184 | tf_op jit(solution)/shard_map/concatenate | solution.py:49
  22.5 4.0 %fusion.100 = (f32[2,2048]{1,0:T(2,128)S(1)}, f32[2,2048,8]{1,2,0:T(8,128)S(1)}) fusion(pred[2,2048,8]{1,2,0:T(8,128)(4,1)S(1)} %gt.33, bf16[2,2048,576]{2,1,0:T(8,128)(2,1)} %bitcast.48, bf16[2,8,576]{2,1,0:T(8,128)(2,1)S(1)} %copy-done.2), kind=kOutput, calls=%fused_computation.114 | convolution fusion | flops 37842944 | bytes 4917248 | tf_op jit(solution)/shard_map/brc,bkc->brk/dot_general | solution.py:69
  26.4 23.1 %fusion = (f32[2,2048]{1,0:T(2,128)S(1)}, f32[2,2048,2048]{1,2,0:T(8,128)}) fusion(pred[2,2048]{1,0:T(4,128)(4,1)S(1)} %broadcast_compare_fusion, bf16[2,2048,576]{2,1,0:T(8,128)(2,1)} %bitcast.49, bf16[2,2048,576]{1,2,0:T(8,128)(2,1)} %param.12), kind=kOutput, calls=%fused_computation.2 | convolution fusion | flops 9688838144 | bytes 43012096 | tf_op jit(solution)/shard_map/brc,bkc->brk/dot_general | solution.py:64
  49.5 25.5 %pmax.7 = f32[2,2048]{1,0:T(2,128)S(1)} all-reduce(f32[2,2048]{1,0:T(2,128)S(1)} %max.5), channel_id=1, replica_groups=mesh['seq'=8,'head'=4] {'seq'}, use_global_device_ids=true, to_apply=%region_2.3 | all-reduce | flops 4096 | bytes 32768 | tf_op jit(solution)/shard_map/pmax | solution.py:75
  75.2 15.7 %fusion.1 = f32[2,2048]{1,0:T(2,128)S(1)} fusion(f32[2,2048,2048]{1,2,0:T(8,128)} %get-tuple-element.6, f32[2,2048]{1,0:T(2,128)S(1)} %pmax.7, pred[2,2048]{1,0:T(4,128)(4,1)S(1)} %broadcast_compare_fusion), kind=kLoop, calls=%fused_computation.3 | loop fusion | flops 41938944 | bytes 33591296 | tf_op jit(solution)/shard_map/reduce_sum | solution.py:78
  90.9 1.1 copy.82
  92.0 1.3 fusion.53
  93.3 23.2 %add_convert_fusion = bf16[2,2048,512]{2,1,0:T(8,128)(2,1)} fusion(f32[2,2048,512]{2,1,0:T(8,128)S(1)} %fusion.53, f32[2,2048,2048]{1,2,0:T(8,128)} %get-tuple-element.6, f32[2,2048]{1,0:T(2,128)S(1)} %pmax.7, pred[2,2048]{1,0:T(4,128)(4,1)S(1)} %broadcast_compare_fusion, bf16[2,2048,576]{1,2,0:T(8,128)(2,1)} %param.12), kind=kOutput, calls=%fused_computation.7 | convolution fusion | flops 8636071936 | bytes 50352128 | tf_op jit(solution)/shard_map/brk,bkl->brl/dot_general | solution.py:79
  116.6 9.0 %reduce-scatter.10.cloned.1.call-done = bf16[256,2]{1,0:T(8,128)(2,1)} async-done(((bf16[2048,2]{1,0:T(8,128)(2,1)}), bf16[256,2]{1,0:T(8,128)(2,1)}) %reduce-scatter.10.cloned.1.call-update) | async-done | bytes 1040
  125.6 0.9 copy.83
  126.5 53.5 %reduce-scatter.6.cloned.1.call-done = bf16[2,256,512]{2,1,0:T(8,128)(2,1)} async-done(((bf16[2,2048,512]{2,1,0:T(8,128)(2,1)}), bf16[2,256,512]{2,1,0:T(8,128)(2,1)}) %reduce-scatter.6.cloned.1.call-update) | async-done | bytes 524304 | tf_op jit(solution)/shard_map/reduce_scatter | solution.py:96
  180.1 1.2 divide_convert_fusion
  181.3 3.1 %fusion.25 = bf16[32,2,1,8,128]{4,3,2,1,0:T(8,128)(2,1)S(1)} fusion(bf16[32,512,128]{2,1,0:T(8,128)(2,1)} %param.19, bf16[2,8,32,512]{3,2,1,0:T(8,128)(2,1)S(1)} %bitcast.52), kind=kOutput, calls=%fused_computation.22 | convolution fusion | flops 67174400 | bytes 4849664 | tf_op jit(solution)/shard_map/bthl,hlv->bthv/dot_general | solution.py:102
  184.4 0.7 copy.89
  185.1 23.5 %all-gather.3.cloned.1.call-done = bf16[2,64,4096]{2,1,0:T(8,128)(2,1)} async-done(((bf16[2,8,4096]{2,1,0:T(8,128)(2,1)}), bf16[2,64,4096]{2,1,0:T(8,128)(2,1)}) %all-gather.3.cloned.1.call-update) | async-done | bytes 1048592 | tf_op jit(solution)/shard_map/all_gather | solution.py:107
  208.6 4.7 %fusion.19 = bf16[2,64,896]{2,1,0:T(8,128)(2,1)S(1)} fusion(bf16[2,64,4096]{2,1,0:T(8,128)(2,1)} %all-gather.3.cloned.1.call-done, bf16[4096,896]{1,0:T(8,128)(2,1)} %param.20), kind=kOutput, calls=%fused_computation.20 | convolution fusion | flops 939638784 | bytes 8617984 | tf_op jit(solution)/shard_map/dot_general | solution.py:106
  213.3 21.0 %all-gather = bf16[8,64,896]{2,1,0:T(8,128)(2,1)S(1)} all-gather(bf16[2,64,896]{2,1,0:T(8,128)(2,1)S(1)} %fusion.19), channel_id=2, replica_groups=mesh['seq'=8,'head'=4] {'head'}, dimensions={0}, use_global_device_ids=true | all-gather | bytes 1146880 | tf_op jit(solution)/shard_map/all_gather | solution.py:112
  234.6 11.8 %psum.7 = f32[2,64]{1,0:T(2,128)S(1)} all-reduce(f32[2,64]{1,0:T(2,128)S(1)} %multiply_reduce_fusion), channel_id=1, replica_groups=mesh['seq'=8,'head'=4] {'seq'}, use_global_device_ids=true, to_apply=%region_9.10 | all-reduce | flops 128 | bytes 1024 | tf_op jit(solution)/shard_map/psum | solution.py:115
  246.4 3.6 %fusion.15 = bf16[2,64,2048]{2,1,0:T(8,128)(2,1)} fusion(bf16[896,2048]{1,0:T(8,128)(2,1)} %param.23, bf16[2,64,896]{2,1,0:T(8,128)(2,1)S(1)} %reduce_sum.41, bf16[2,64,896]{2,1,0:T(8,128)(2,1)S(1)} %copy-done, f32[896]{0:T(1024)S(1)} %convert_element_type.68, f32[2,64]{1,0:T(2,128)S(1)} %add_rsqrt_fusion), kind=kOutput, calls=%fused_computation.17 | convolution fusion | flops 470712320 | bytes 4657152 | tf_op jit(solution)/shard_map/dot_general | solution.py:119
  250.1 33.7 %reduce-scatter.8.cloned.1.call-done = bf16[2,64,256]{2,1,0:T(8,128)(2,1)} async-done(((bf16[2,64,2048]{2,1,0:T(8,128)(2,1)}), bf16[2,64,256]{2,1,0:T(8,128)(2,1)}) %reduce-scatter.8.cloned.1.call-update) | async-done | bytes 65552 | tf_op jit(solution)/shard_map/reduce_scatter | solution.py:120
  (36 shorter events, 1.3 us)
Async XLA Ops:
  6.5 119.1 %reduce-scatter.10.cloned.1.call-start = ((), (), s32[]{:S(2)}) async-start(), calls=%async_computation.6 | async-start | bytes 589824
  14.4 1.2 copy-start.1
  16.1 6.3 %copy-start.4 = (s32[2]{0:T(128)S(1)}, s32[2]{0:T(128)}, u32[]{:S(2)}) copy-start(s32[2]{0:T(128)} %param.17) | copy-start | bytes 28
  16.1 6.4 %copy-start.2 = (bf16[2,8,576]{2,1,0:T(8,128)(2,1)S(1)}, bf16[2,8,576]{2,1,0:T(8,128)(2,1)}, u32[]{:S(2)}) copy-start(bf16[2,8,576]{2,1,0:T(8,128)(2,1)} %param.13) | copy-start | bytes 55300
  92.0 88.1 %reduce-scatter.6.cloned.1.call-start = ((), (), s32[]{:S(2)}) async-start(), calls=%async_computation.3 | async-start | bytes 4718592 | tf_op jit(solution)/shard_map/reduce_scatter | solution.py:96
  116.5 68.6 %copy-start.3 = (bf16[896]{0:T(1024)(128)(2,1)S(1)}, bf16[896]{0:T(1024)(128)(2,1)}, u32[]{:S(2)}) copy-start(bf16[896]{0:T(1024)(128)(2,1)} %param.22) | copy-start | bytes 5380
  116.5 92.1 %all-gather.3.cloned.1.call-start = ((), (), s32[]{:S(2)}) async-start(), calls=%async_computation.4 | async-start | bytes 1179648 | tf_op jit(solution)/shard_map/all_gather | solution.py:107
  184.4 50.1 %copy-start = (bf16[2,64,896]{2,1,0:T(8,128)(2,1)S(1)}, bf16[2,64,896]{2,1,0:T(8,128)(2,1)}, u32[]{:S(2)}) copy-start(bf16[2,64,896]{2,1,0:T(8,128)(2,1)} %param.21) | copy-start | bytes 688132
  185.1 98.7 %reduce-scatter.8.cloned.1.call-start = ((), (), s32[]{:S(2)}) async-start(), calls=%async_computation.5 | async-start | bytes 589824 | tf_op jit(solution)/shard_map/reduce_scatter | solution.py:120
Sparse Core Ops, SparseCore 0:
  92.1 33.5 reduce-scatter.9
  129.0 51.0 reduce-scatter.5
  185.2 23.3 all-gather.2
  250.2 33.5 reduce-scatter.7
